TPU v7x, 256 devices: a whole 4x4x8 slice. The times are simulated.
256 devices in a mesh: dp: 4 (over y_lo, core), sp: 8 (over y_hi, x), tp: 8 (over z).
Axes of the slice: x: 4, y: 4 (y_hi: 2, y_lo: 2; y = y_hi * 2 + y_lo), z: 8, core: 2. Of those that a mesh axis runs over, the one named last changes fastest.
Arguments:
- query: bfloat16 [4, 3072, 3072], P('dp', 'sp', 'tp'), may hold values from -110 to 110
- key: bfloat16 [4, 3072, 3072], P('dp', 'sp', 'tp'), may hold values from -8 to 8
- value: bfloat16 [4, 3072, 3072], P('dp', 'sp', 'tp'), may hold values from -6 to 6
- text_key: bfloat16 [4, 256, 3072], P('dp', None, 'tp'), may hold values from -6 to 6
- text_value: bfloat16 [4, 256, 3072], P('dp', None, 'tp'), may hold values from -6 to 6
- grad_out: bfloat16 [4, 3072, 3072], P('dp', 'sp', 'tp'), may hold values from -6 to 6
- gate: bfloat16 [4, 3072], P('dp'), may hold values from 0.5 to 1.5
- out_weight: bfloat16 [3072, 3072], P('tp', 'dp'), may hold values from -0.109375 to 0.109375
- windows: int32 [8, 2], P('sp'), may hold values from 0 to 2, as said below
- tile_map: int32 [8, 1], replicated, may hold values from 0 to 2, as said below
- text_count: int32 [4], P('dp'), may hold values from 1 to 256
Outputs:
- grad_query: bfloat16 [4, 3072, 3072], P('dp', 'sp', 'tp')
- grad_key: bfloat16 [4, 3072, 3072], P('dp', 'sp', 'tp')
- grad_value: bfloat16 [4, 3072, 3072], P('dp', 'sp', 'tp')
- grad_text_key: bfloat16 [4, 256, 3072], P('dp', None, 'tp')
- grad_text_value: bfloat16 [4, 256, 3072], P('dp', None, 'tp')
- grad_weight: float32 [3072, 3072], P('tp', 'dp')
Inputs may be any that keep to these rules, and one draw needn't show every extreme that they name: `tile_map`: the positions within each row are distinct. `windows`: the time reach is 0 or 1; the first tile of every time slab has time reach 1 and spatial reach 2.
All inputs are finite; a program needn't handle non-finite values.
Results may differ from a plain program's by a relative error of at most 0.024.
Values may be sent and summed in bfloat16 or wider, within the bound.
A program may use at most 64 MiB of HBM per device.

v0:
```python
import jax
import jax.numpy as jnp
from jax import lax
from jax.sharding import PartitionSpec as P

HD = 128
TILE = 384


def in_order(parts, dim):
    shape = list(parts.shape[1:])
    shape[dim] *= parts.shape[0]
    return jnp.moveaxis(parts, 0, dim).reshape(shape)


def from_everyone(shard, axis):
    copies = jnp.broadcast_to(shard, (lax.axis_size(axis), *shard.shape))
    return lax.all_to_all(copies, axis, split_axis=0, concat_axis=0, tiled=True)


def gathered_copies(shard, axis, dim):
    return in_order(from_everyone(shard, axis), dim)


def padded(cells, sides, width):
    for axis, dim in sides:
        count = lax.axis_size(axis)
        ends = count - 1
        head = lax.slice_in_dim(cells, 0, width, axis=dim)
        tail = lax.slice_in_dim(cells, cells.shape[dim] - width, cells.shape[dim], axis=dim)
        cells = jnp.concatenate(
            [
                lax.ppermute(tail, axis, [(i, (i + 1) % count) for i in range(ends)]),
                cells,
                lax.ppermute(head, axis, [((i + 1) % count, i) for i in range(ends)]),
            ],
            axis=dim,
        )
    return cells


def shifted(block, axis, distance):
    devices = range(lax.axis_size(axis))
    route = [(i - distance, i) for i in devices if i - distance in devices]
    return lax.ppermute(block, axis, route)


def cut_along(shard, dim, count):
    shape = shard.shape
    parts = shard.reshape(*shape[:dim], count, shape[dim] // count, *shape[dim + 1 :])
    return jnp.moveaxis(parts, dim, 0)


def summed_on_arrival(shard, axis, dim):
    count = lax.axis_size(axis)
    parts = lax.all_to_all(cut_along(shard, dim, count), axis, 0, 0, tiled=True)
    return jnp.sum(parts.astype(jnp.float32), axis=0)


def window_mask(own_map, side_maps, valid, spans, text_live):
    reach = jnp.abs(jnp.arange(3, dtype=jnp.int32) - 1)
    near_time = reach[None, :, None] <= spans[:, 0][:, None, None]
    near_space = (
        jnp.abs(own_map[:, None, None] - side_maps[None, :, :]) <= spans[:, 1][:, None, None]
    )
    allowed = near_time & near_space & valid[None, :, None]
    count = own_map.shape[0]
    tiles = allowed.reshape(count, 3 * count)
    video = jnp.broadcast_to(tiles[:, None, :, None], (count, TILE, 3 * count, TILE))
    video = video.reshape(count * TILE, 3 * count * TILE)
    text = jnp.broadcast_to(text_live[None, :], (count * TILE, text_live.shape[0]))
    return jnp.concatenate([video, text], axis=1)


def tile_attention(query, keys, values, grad_attn, allowed):
    factor = HD ** (-0.5)
    scores = factor * jnp.dot(query, keys.T, preferred_element_type=jnp.float32)
    scores = jnp.where(allowed, scores, -1e30)
    top = jnp.max(scores, axis=1, keepdims=True)
    weights = jnp.exp(scores - top)
    weights = weights / jnp.sum(weights, axis=1, keepdims=True)
    probs = weights.astype(jnp.bfloat16)
    attended = jnp.dot(probs, values, preferred_element_type=jnp.float32).astype(jnp.bfloat16)
    delta = jnp.sum(
        grad_attn.astype(jnp.float32) * attended.astype(jnp.float32), axis=1, keepdims=True
    )
    grad_probs = jnp.dot(grad_attn, values.T, preferred_element_type=jnp.float32)
    grad_scores = (weights * (grad_probs - delta)).astype(jnp.bfloat16)
    grad_query = factor * jnp.dot(grad_scores, keys, preferred_element_type=jnp.float32)
    grad_keys = factor * jnp.dot(grad_scores.T, query, preferred_element_type=jnp.float32)
    grad_values = jnp.dot(probs.T, grad_attn, preferred_element_type=jnp.float32)
    return (attended, grad_query, grad_keys, grad_values)


def per_device(
    query,
    key,
    value,
    text_key,
    text_value,
    grad_out,
    gate,
    out_weight,
    windows,
    tile_map,
    text_count,
):
    own_query = query[0]
    tok = own_query.shape[0]
    width = own_query.shape[1]
    full_grad = lax.all_gather(grad_out[0], "tp", axis=1, tiled=True)
    scaled = (full_grad.astype(jnp.float32) * gate[0].astype(jnp.float32)[None, :]).astype(
        jnp.bfloat16
    )
    grad_attn = lax.dot_general(
        scaled,
        gathered_copies(out_weight, "dp", 1),
        (((1,), (1,)), ((), ())),
        preferred_element_type=jnp.float32,
    )
    grad_attn = grad_attn.astype(jnp.bfloat16)
    paired = jnp.stack([key[0], value[0]], axis=0)
    extended = padded(paired, (("sp", 1),), tok)
    index = lax.axis_index("sp")
    slabs = lax.axis_size("sp")
    tiles_here = tile_map.shape[1]
    blank = jnp.zeros((1, tiles_here), jnp.int32)
    padded_map = jnp.concatenate([blank, tile_map, blank], axis=0)
    own_map = lax.dynamic_index_in_dim(tile_map, index, 0, keepdims=False)
    side_maps = lax.dynamic_slice_in_dim(padded_map, index, 3, 0)
    others = index + jnp.arange(3, dtype=jnp.int32) - 1
    valid = (others >= 0) & (others < slabs)
    text_live = jnp.arange(text_key.shape[1], dtype=jnp.int32) < text_count[0]
    allowed = window_mask(own_map, side_maps, valid, windows, text_live)
    results = [[], [], [], []]
    for head in range(width // HD):
        lower = head * HD
        upper = lower + HD
        all_k = jnp.concatenate([extended[0][:, lower:upper], text_key[0][:, lower:upper]], axis=0)
        all_v = jnp.concatenate(
            [extended[1][:, lower:upper], text_value[0][:, lower:upper]], axis=0
        )
        outcome = tile_attention(
            own_query[:, lower:upper], all_k, all_v, grad_attn[:, lower:upper], allowed
        )
        for place in range(4):
            results[place].append(outcome[place])
    attended = jnp.concatenate(results[0], axis=1)
    grad_q = jnp.concatenate(results[1], axis=1)
    grad_k = jnp.concatenate(results[2], axis=1)
    grad_v = jnp.concatenate(results[3], axis=1)
    earlier = jnp.stack([grad_k[:tok], grad_v[:tok]], axis=0)
    later = jnp.stack([grad_k[2 * tok : 3 * tok], grad_v[2 * tok : 3 * tok]], axis=0)
    from_later = shifted(earlier.astype(jnp.bfloat16), "sp", -1).astype(earlier.dtype)
    from_earlier = shifted(later.astype(jnp.bfloat16), "sp", 1).astype(later.dtype)
    own_k = grad_k[tok : 2 * tok] + from_later[0] + from_earlier[0]
    own_v = grad_v[tok : 2 * tok] + from_later[1] + from_earlier[1]
    text_k, text_v = (
        lax.psum(grad_k[3 * tok :].astype(jnp.bfloat16), "sp").astype(jnp.float32),
        lax.psum(grad_v[3 * tok :].astype(jnp.bfloat16), "sp").astype(jnp.float32),
    )
    local_weight = lax.dot_general(
        attended, scaled, (((0,), (0,)), ((), ())), preferred_element_type=jnp.float32
    )
    spread = summed_on_arrival(local_weight.astype(jnp.bfloat16), ("dp", "sp"), 1)
    weight_grad = gathered_copies(spread, "sp", 1)
    return (
        grad_q.astype(jnp.bfloat16)[None],
        own_k.astype(jnp.bfloat16)[None],
        own_v.astype(jnp.bfloat16)[None],
        text_k.astype(jnp.bfloat16)[None],
        text_v.astype(jnp.bfloat16)[None],
        weight_grad,
    )


def solution(mesh):
    placed = (
        P("dp", "sp", "tp"),
        P("dp", "sp", "tp"),
        P("dp", "sp", "tp"),
        P("dp", None, "tp"),
        P("dp", None, "tp"),
        P("dp", "sp", "tp"),
        P("dp", None),
        P("tp", "dp"),
        P("sp", None),
        P(),
        P("dp"),
    )
    return jax.shard_map(
        per_device,
        mesh=mesh,
        in_specs=placed,
        out_specs=(
            P("dp", "sp", "tp"),
            P("dp", "sp", "tp"),
            P("dp", "sp", "tp"),
            P("dp", None, "tp"),
            P("dp", None, "tp"),
            P("tp", "dp"),
        ),
        check_vma=False,
    )
```

profile of v0, /device:TPU:32, one launch (start us, length us, event | category | flops | bytes accessed | tf_op | source)
XLA Modules:
  0.0 227.6 jit_solution(2305887054889296009)
XLA Ops:
  7.2 1.0 constant_dynamic-update-slice_fusion.1
  8.2 1.0 constant_dynamic-update-slice_fusion
  9.2 1.3 collective-permute-start.1
  10.5 4.6 %collective-permute-start = (bf16[2,384,384]{2,1,0:T(8,128)(2,1)S(1)}, bf16[2,384,384]{2,1,0:T(8,128)(2,1)S(1)}, u32[]{:S(2)}, u32[]{:S(2)}) collective-permute-start(bf16[2,384,384]{2,1,0:T(8,128)(2,1)S(1)} %constant_dynamic-update-slice_fusion), channel_id=1, source_target_pairs={{0,8},{8,16},{16,24},{24,32},{32,40},{40,48},{48,56},{1,9},{9,17},... | collective-permute-start | bytes 1769480 | tf_op jit(solution)/shard_map/ppermute | solution.py:33
  15.1 1.4 copy.25
  16.4 1.7 broadcast_in_dim.59
  18.1 4.6 %all-to-all-start = ((bf16[4,384,768]{1,2,0:T(8,128)(2,1)}), bf16[4,384,768]{1,2,0:T(8,128)(2,1)}, u32[]{:S(2)}, u32[]{:S(2)}) async-start(bf16[4,384,768]{1,2,0:T(8,128)(2,1)} %broadcast_in_dim.59), calls=%async_computation | async-start | bytes 4718592 | tf_op jit(solution)/shard_map/all_to_all | solution.py:18
  22.8 0.7 all-gather.3.cloned.1.call-update
  24.2 0.6 fusion.82
  24.8 0.6 constant_dynamic-slice_fusion
  25.4 2.0 fusion.62
  28.1 1.0 fusion.78
  29.2 0.5 fusion.84
  29.7 0.4 fusion.19
  30.1 0.5 fusion.85
  31.1 0.5 fusion.83
  32.4 1.1 convolution_convert_fusion.2
  33.9 1.0 copy-done.15
  34.9 1.1 convolution_convert_fusion.1
  35.9 1.3 fusion.33
  37.3 23.3 %all-to-all-done = bf16[4,384,768]{1,2,0:T(8,128)(2,1)} async-done(((bf16[4,384,768]{1,2,0:T(8,128)(2,1)}), bf16[4,384,768]{1,2,0:T(8,128)(2,1)}, u32[]{:S(2)}, u32[]{:S(2)}) %all-to-all-start) | async-done | bytes 2359328 | tf_op jit(solution)/shard_map/all_to_all | solution.py:18
  60.5 11.3 %all-gather.3.cloned.1.call-done = bf16[1,384,3072]{2,1,0:T(8,128)(2,1)} async-done(((bf16[1,384,384]{2,1,0:T(8,128)(2,1)}), bf16[1,384,3072]{2,1,0:T(8,128)(2,1)}) %all-gather.3.cloned.1.call-update) | async-done | bytes 2359312 | tf_op jit(solution)/shard_map/all_gather | solution.py:111
  71.8 4.0 %fusion.22 = bf16[384,384]{0,1:T(8,128)(2,1)S(1)} fusion(bf16[384,3072]{0,1:T(8,128)(2,1)} %bitcast.12, bf16[1,384,3072]{2,1,0:T(8,128)(2,1)} %all-gather.3.cloned.1.call-done, f32[3072]{0:T(1024)S(1)} %bitcast.122), kind=kOutput, calls=%fused_computation.38 | convolution fusion | flops 909656064 | bytes 5025792 | tf_op jit(solution)/shard_map/dot_general | solution.py:115
  75.8 0.4 fusion.53
  76.3 1.3 fusion.56
  77.6 1.3 fusion.59
  78.9 0.4 multiply_reduce_fusion.2
  79.5 0.6 fusion.10
  80.4 1.6 fusion.11
  82.3 1.6 fusion.12
  83.9 2.2 convolution_multiply_fusion.3
  86.1 1.4 convolution_convert_fusion
  87.5 2.5 %copy.29 = bf16[384,3072]{0,1:T(8,128)(2,1)} copy(bf16[384,3072]{1,0:T(8,128)(2,1)S(1)} %convolution_convert_fusion) | data formatting | bytes 4718592 | tf_op jit(solution)/shard_map/convert_element_type | solution.py:165
  90.0 7.3 %all-to-all-start.1 = ((bf16[32,384,96]{1,2,0:T(8,128)(2,1)}), bf16[32,384,96]{1,2,0:T(8,128)(2,1)S(1)}, u32[]{:S(2)}, u32[]{:S(2)}) async-start(bf16[32,384,96]{1,2,0:T(8,128)(2,1)} %bitcast.112), calls=%async_computation.1 | async-start | bytes 4718592 | tf_op jit(solution)/shard_map/all_to_all | solution.py:56
  97.3 1.5 fusion.76
  99.0 0.5 convolution_multiply_fusion.4
  99.5 0.7 copy-done.18
  100.2 0.5 convolution_multiply_fusion.5
  101.2 0.4 copy-done.10
  101.6 0.9 pad_maximum_fusion.4
  102.5 4.5 %collective-permute-start.3 = (bf16[2,384,384]{1,2,0:T(8,128)(2,1)}, bf16[2,384,384]{1,2,0:T(8,128)(2,1)}, u32[]{:S(2)}, u32[]{:S(2)}) collective-permute-start(bf16[2,384,384]{1,2,0:T(8,128)(2,1)} %pad_maximum_fusion.4), channel_id=1, source_target_pairs={{0,8},{8,16},{16,24},{24,32},{32,40},{40,48},{48,56},{1,9},{9,17},... | collective-permute-start | bytes 1769480 | tf_op jit(solution)/shard_map/ppermute | solution.py:45
  107.0 0.9 pad_maximum_fusion.3
  107.9 1.3 collective-permute-start.2
  109.2 0.7 slice_bitcast_fusion.11
  109.9 0.7 slice_bitcast_fusion.10
  110.6 1.8 fusion.28
  112.4 1.5 pad_maximum_fusion.1
  113.9 14.7 %all-to-all-done.1 = bf16[32,384,96]{1,2,0:T(8,128)(2,1)S(1)} async-done(((bf16[32,384,96]{1,2,0:T(8,128)(2,1)}), bf16[32,384,96]{1,2,0:T(8,128)(2,1)S(1)}, u32[]{:S(2)}, u32[]{:S(2)}) %all-to-all-start.1) | async-done | bytes 2359328 | tf_op jit(solution)/shard_map/all_to_all | solution.py:56
  129.0 1.1 broadcast_in_dim.64
  130.1 6.7 %all-to-all-start.2 = ((f32[8,384,96]{1,2,0:T(8,128)}), f32[8,384,96]{1,2,0:T(8,128)S(1)}, u32[]{:S(2)}, u32[]{:S(2)}) async-start(f32[8,384,96]{1,2,0:T(8,128)} %broadcast_in_dim.64), calls=%async_computation.2 | async-start | bytes 2359296 | tf_op jit(solution)/shard_map/all_to_all | solution.py:18
  136.8 1.9 fusion.29
  138.7 1.7 fusion.30
  140.4 0.7 pad_maximum_fusion.11
  141.1 1.8 copy.30
  143.0 1.5 pad_maximum_fusion
  144.5 65.8 %all-reduce.3.cloned.1.call-done = (bf16[1,256,384]{1,2,0:T(8,128)(2,1)}, bf16[1,256,384]{1,2,0:T(8,128)(2,1)}) async-done(((bf16[1,256,384]{1,2,0:T(8,128)(2,1)}, bf16[1,256,384]{1,2,0:T(8,128)(2,1)}), (bf16[1,256,384]{1,2,0:T(8,128)(2,1)}, bf16[1,256,384]{1,2,0:T(8,128)(2,1)})) %all-reduce.3.cloned.1.call-update) | async-done | bytes 393232 | tf_op jit(solution)/shard_map/psum | solution.py:159
  210.3 1.7 copy.33
  212.0 1.7 copy.34
  213.8 1.1 convert_element_type.109
  214.9 1.1 convert_element_type.108
  216.1 1.5 fusion.41
  217.6 0.9 copy.31
  218.4 0.9 copy.32
  219.3 1.4 copy.35
  (105 shorter events, 4.0 us)
Async XLA Ops:
  9.2 18.5 %collective-permute-start.1 = (bf16[2,384,384]{2,1,0:T(8,128)(2,1)S(1)}, bf16[2,384,384]{2,1,0:T(8,128)(2,1)S(1)}, u32[]{:S(2)}, u32[]{:S(2)}) collective-permute-start(bf16[2,384,384]{2,1,0:T(8,128)(2,1)S(1)} %constant_dynamic-update-slice_fusion), channel_id=1, source_target_pairs={{8,0},{16,8},{24,16},{32,24},{40,32},{48,40},{56,48},{9,1},{17,9},... | collective-permute-start | bytes 1769480 | tf_op jit(solution)/shard_map/ppermute | solution.py:35
  10.5 17.2 %collective-permute-start = (bf16[2,384,384]{2,1,0:T(8,128)(2,1)S(1)}, bf16[2,384,384]{2,1,0:T(8,128)(2,1)S(1)}, u32[]{:S(2)}, u32[]{:S(2)}) collective-permute-start(bf16[2,384,384]{2,1,0:T(8,128)(2,1)S(1)} %constant_dynamic-update-slice_fusion), channel_id=1, source_target_pairs={{0,8},{8,16},{16,24},{24,32},{32,40},{40,48},{48,56},{1,9},{9,17},... | collective-permute-start | bytes 1769480 | tf_op jit(solution)/shard_map/ppermute | solution.py:33
  18.1 6.1 %copy-start.36 = (s32[1,2]{1,0:T(1,128)S(1)}, s32[1,2]{1,0:T(1,128)}, u32[]{:S(2)}) copy-start(s32[1,2]{1,0:T(1,128)} %param.19) | copy-start | bytes 28
  18.1 6.7 %copy-start.38 = (s32[8,1]{0,1:T(1,128)S(1)}, s32[8,1]{0,1:T(1,128)}, u32[]{:S(2)}) copy-start(s32[8,1]{0,1:T(1,128)} %param.20) | copy-start | bytes 100
  18.1 9.3 %copy-start.35 = (bf16[1,3072]{1,0:T(2,128)(2,1)S(1)}, bf16[1,3072]{1,0:T(2,128)(2,1)}, u32[]{:S(2)}) copy-start(bf16[1,3072]{1,0:T(2,128)(2,1)} %param.17) | copy-start | bytes 18436
  18.1 9.5 %copy-start.29 = (bf16[1,256,384]{2,1,0:T(8,128)(2,1)S(1)}, bf16[1,256,384]{2,1,0:T(8,128)(2,1)}, u32[]{:S(2)}) copy-start(bf16[1,256,384]{2,1,0:T(8,128)(2,1)} %param.14) | copy-start | bytes 589828
  18.1 9.5 %copy-start.30 = (bf16[1,256,384]{2,1,0:T(8,128)(2,1)S(1)}, bf16[1,256,384]{2,1,0:T(8,128)(2,1)}, u32[]{:S(2)}) copy-start(bf16[1,256,384]{2,1,0:T(8,128)(2,1)} %param.15) | copy-start | bytes 589828
  18.1 42.4 %all-to-all-start = ((bf16[4,384,768]{1,2,0:T(8,128)(2,1)}), bf16[4,384,768]{1,2,0:T(8,128)(2,1)}, u32[]{:S(2)}, u32[]{:S(2)}) async-start(bf16[4,384,768]{1,2,0:T(8,128)(2,1)} %broadcast_in_dim.59), calls=%async_computation | async-start | bytes 4718592 | tf_op jit(solution)/shard_map/all_to_all | solution.py:18
  22.8 49.1 %all-gather.3.cloned.1.call-start = ((), (), s32[]{:S(2)}) async-start(), calls=%async_computation.3 | async-start | bytes 2654208 | tf_op jit(solution)/shard_map/all_gather | solution.py:111
  27.6 1.5 copy-start.31
  27.6 2.5 %copy-start.32 = (bf16[256,128]{1,0:T(8,128)(2,1)}, bf16[256,128]{1,0:T(8,128)(2,1)S(1)}, u32[]{:S(2)}) copy-start(bf16[256,128]{1,0:T(8,128)(2,1)S(1)} %get-tuple-element.40) | copy-start | bytes 196612
  27.7 6.2 %copy-start.33 = (bf16[256,128]{1,0:T(8,128)(2,1)}, bf16[256,128]{1,0:T(8,128)(2,1)S(1)}, u32[]{:S(2)}) copy-start(bf16[256,128]{1,0:T(8,128)(2,1)S(1)} %get-tuple-element.37) | copy-start | bytes 196612
  28.1 1.1 copy-start.27
  29.1 1.0 copy-start.21
  29.1 1.9 copy-start.20
  29.1 3.3 %copy-start.23 = (bf16[1152,128]{1,0:T(8,128)(2,1)}, bf16[1152,128]{1,0:T(8,128)(2,1)S(1)}, u32[]{:S(2)}) copy-start(bf16[1152,128]{1,0:T(8,128)(2,1)S(1)} %get-tuple-element.32) | copy-start | bytes 884740
  29.1 4.7 %copy-start.25 = (bf16[1152,128]{1,0:T(8,128)(2,1)}, bf16[1152,128]{1,0:T(8,128)(2,1)S(1)}, u32[]{:S(2)}) copy-start(bf16[1152,128]{1,0:T(8,128)(2,1)S(1)} %get-tuple-element.31) | copy-start | bytes 884740
  30.7 2.8 %copy-start.2 = (f32[384,1408]{0,1:T(8,128)}, f32[384,1408]{0,1:T(8,128)S(1)}, u32[]{:S(2)}) copy-start(f32[384,1408]{0,1:T(8,128)S(1)} %get-tuple-element.50) | copy-start | bytes 6488068
  31.6 4.3 %copy-start = (f32[384,1408]{0,1:T(8,128)}, f32[384,1408]{0,1:T(8,128)S(1)}, u32[]{:S(2)}) copy-start(f32[384,1408]{0,1:T(8,128)S(1)} %get-tuple-element.46) | copy-start | bytes 6488068
  32.0 1.9 copy-start.13
  33.9 1.0 copy-start.15
  71.8 4.0 %copy-start.16 = (bf16[384,1408]{0,1:T(8,128)(2,1)S(1)}, bf16[384,1408]{0,1:T(8,128)(2,1)}, u32[]{:S(2)}) copy-start(bf16[384,1408]{0,1:T(8,128)(2,1)} %copy-done.15) | copy-start | bytes 3244036
  71.8 4.4 %copy-start.14 = (bf16[384,1408]{0,1:T(8,128)(2,1)S(1)}, bf16[384,1408]{0,1:T(8,128)(2,1)}, u32[]{:S(2)}) copy-start(bf16[384,1408]{0,1:T(8,128)(2,1)} %copy-done.13) | copy-start | bytes 3244036
  75.8 1.8 copy-start.12
  76.3 2.6 %copy-start.22 = (bf16[1152,128]{1,0:T(8,128)(2,1)S(1)}, bf16[1152,128]{1,0:T(8,128)(2,1)}, u32[]{:S(2)}) copy-start(bf16[1152,128]{1,0:T(8,128)(2,1)} %get-tuple-element.33) | copy-start | bytes 884740
  76.3 2.6 %copy-start.39 = (bf16[384,128]{0,1:T(8,128)(2,1)S(1)}, bf16[384,128]{0,1:T(8,128)(2,1)}, u32[]{:S(2)}) copy-start(bf16[384,128]{0,1:T(8,128)(2,1)} %convolution_convert_fusion.2) | copy-start | bytes 294916
  76.3 2.6 %copy-start.40 = (bf16[384,128]{0,1:T(8,128)(2,1)S(1)}, bf16[384,128]{0,1:T(8,128)(2,1)}, u32[]{:S(2)}) copy-start(bf16[384,128]{0,1:T(8,128)(2,1)} %convolution_convert_fusion.1) | copy-start | bytes 294916
  77.6 1.9 copy-start.3
  77.6 1.9 copy-start.26
  77.6 1.9 copy-start.34
  79.5 1.0 copy-start.24
  80.1 3.8 %copy-start.19 = (bf16[384,1408]{0,1:T(8,128)(2,1)}, bf16[384,1408]{0,1:T(8,128)(2,1)S(1)}, u32[]{:S(2)}) copy-start(bf16[384,1408]{0,1:T(8,128)(2,1)S(1)} %fusion.10) | copy-start | bytes 3244036
  80.4 1.8 copy-start.1
  82.3 3.8 %copy-start.37 = (bf16[1,384,3072]{2,1,0:T(8,128)(2,1)S(1)}, bf16[1,384,3072]{2,1,0:T(8,128)(2,1)}, u32[]{:S(2)}) copy-start(bf16[1,384,3072]{2,1,0:T(8,128)(2,1)} %all-gather.3.cloned.1.call-done) | copy-start | bytes 7077892
  90.0 38.7 %all-to-all-start.1 = ((bf16[32,384,96]{1,2,0:T(8,128)(2,1)}), bf16[32,384,96]{1,2,0:T(8,128)(2,1)S(1)}, u32[]{:S(2)}, u32[]{:S(2)}) async-start(bf16[32,384,96]{1,2,0:T(8,128)(2,1)} %bitcast.112), calls=%async_computation.1 | async-start | bytes 4718592 | tf_op jit(solution)/shard_map/all_to_all | solution.py:56
  97.3 113.0 %all-reduce.3.cloned.1.call-start = ((), (), s32[]{:S(2)}) async-start(), calls=%async_computation.4 | async-start | bytes 786432 | tf_op jit(solution)/shard_map/psum | solution.py:159
  97.3 1.7 copy-start.17
  97.3 1.7 copy-start.28
  98.9 1.3 copy-start.18
  99.0 1.6 copy-start.6
  100.2 0.9 copy-start.8
  100.7 0.9 copy-start.10
  102.5 111.3 %collective-permute-start.3 = (bf16[2,384,384]{1,2,0:T(8,128)(2,1)}, bf16[2,384,384]{1,2,0:T(8,128)(2,1)}, u32[]{:S(2)}, u32[]{:S(2)}) collective-permute-start(bf16[2,384,384]{1,2,0:T(8,128)(2,1)} %pad_maximum_fusion.4), channel_id=1, source_target_pairs={{0,8},{8,16},{16,24},{24,32},{32,40},{40,48},{48,56},{1,9},{9,17},... | collective-permute-start | bytes 1769480 | tf_op jit(solution)/shard_map/ppermute | solution.py:45
  107.9 107.0 %collective-permute-start.2 = (bf16[2,384,384]{1,2,0:T(8,128)(2,1)}, bf16[2,384,384]{1,2,0:T(8,128)(2,1)}, u32[]{:S(2)}, u32[]{:S(2)}) collective-permute-start(bf16[2,384,384]{1,2,0:T(8,128)(2,1)} %pad_maximum_fusion.3), channel_id=1, source_target_pairs={{8,0},{16,8},{24,16},{32,24},{40,32},{48,40},{56,48},{9,1},{17,9},... | collective-permute-start | bytes 1769480 | tf_op jit(solution)/shard_map/ppermute | solution.py:45
  110.6 1.8 copy-start.4
  110.6 1.8 copy-start.5
  130.1 89.3 %all-to-all-start.2 = ((f32[8,384,96]{1,2,0:T(8,128)}), f32[8,384,96]{1,2,0:T(8,128)S(1)}, u32[]{:S(2)}, u32[]{:S(2)}) async-start(f32[8,384,96]{1,2,0:T(8,128)} %broadcast_in_dim.64), calls=%async_computation.2 | async-start | bytes 2359296 | tf_op jit(solution)/shard_map/all_to_all | solution.py:18
  136.8 6.2 %copy-start.7 = (f32[1408,128]{0,1:T(8,128)S(1)}, f32[1408,128]{0,1:T(8,128)}, u32[]{:S(2)}) copy-start(f32[1408,128]{0,1:T(8,128)} %convolution_multiply_fusion.3) | copy-start | bytes 2162692
  136.8 6.2 %copy-start.9 = (f32[1408,128]{0,1:T(8,128)S(1)}, f32[1408,128]{0,1:T(8,128)}, u32[]{:S(2)}) copy-start(f32[1408,128]{0,1:T(8,128)} %copy-done.8) | copy-start | bytes 2162692
  136.8 6.2 %copy-start.11 = (f32[1408,128]{0,1:T(8,128)S(1)}, f32[1408,128]{0,1:T(8,128)}, u32[]{:S(2)}) copy-start(f32[1408,128]{0,1:T(8,128)} %copy-done.10) | copy-start | bytes 2162692
Sparse Core Ops, SparseCore 0:
  25.4 46.3 all-gather.2
  110.7 99.5 all-reduce.2
where the time goes:
time: 229 us; the launch traced here: 228 us
  waiting for transfers between devices  116 us (51%)
  starting transfers between devices  30.3 us (13%)
  matrix products  24.9 us (11%)
  local copies, waits for them, and re-layouts  24.4 us (11%)
  other arithmetic  16.9 us (7%)
  between operations  15.2 us (7%)
    psum x1, waiting for transfers between devices, per_device(): lax.psum(grad_k[3 * tok:].astype(jnp.bfloat16), 'sp').astype(jnp.float32)  65.8 us
    all_to_all x2, waiting for transfers between devices, from_everyone(): return lax.all_to_all(copies, axis, split_axis=0, concat_axis=0, tiled=True)  23.3 us
    all_to_all x1, waiting for transfers between devices, summed_on_arrival(): parts = lax.all_to_all(cut_along(shard, dim, count), axis, 0, 0, tiled=True)  14.7 us
    unnamed x90, local copies, waits for them, and re-layouts  14.2 us
    all_to_all x2, starting transfers between devices, from_everyone(): return lax.all_to_all(copies, axis, split_axis=0, concat_axis=0, tiled=True)  11.3 us
    all_gather x1, waiting for transfers between devices, per_device(): full_grad = lax.all_gather(grad_out[0], 'tp', axis=1, tiled=True)  11.3 us
    all_to_all x1, starting transfers between devices, summed_on_arrival(): parts = lax.all_to_all(cut_along(shard, dim, count), axis, 0, 0, tiled=True)  7.3 us
    ppermute x2, starting transfers between devices, shifted(): return lax.ppermute(block, axis, route)  5.78 us
  transfers between devices with their start and end apart: 9, of which 4 were waited for; matrix products, arithmetic and copies ran while one was open for 19% of the time, Pallas kernels for 0%

commit v1 on v0

--- a/solution.py
+++ b/solution.py
@@ -2,9 +2,17 @@
 import jax.numpy as jnp
 from jax import lax
 from jax.sharding import PartitionSpec as P
+from jax.lax import all_to_all, axis_size
 
 HD = 128
 TILE = 384
+
+
+def do_blocks(mine):
+    current_value = all_to_all(
+        jnp.stack([mine for _ in range(axis_size("tp"))], axis=0), "tp", 0, 0
+    )
+    return jnp.concatenate(current_value, 1)
 
 
 def in_order(parts, dim):
@@ -108,7 +116,7 @@
     own_query = query[0]
     tok = own_query.shape[0]
     width = own_query.shape[1]
-    full_grad = lax.all_gather(grad_out[0], "tp", axis=1, tiled=True)
+    full_grad = do_blocks(grad_out[0])
     scaled = (full_grad.astype(jnp.float32) * gate[0].astype(jnp.float32)[None, :]).astype(
         jnp.bfloat16
     )

time: 229 us -> 298 us (1.30)
  waiting for transfers between devices: 116 us -> 155 us
  local copies, waits for them, and re-layouts: 24.4 us -> 37.1 us
  starting transfers between devices: 30.3 us -> 40 us
  other arithmetic: 16.9 us -> 24.5 us
    all_to_all x0 -> x1, waiting for transfers between devices: none -> 32.8 us  [do_blocks(): all_to_all(jnp.stack([mine for _ in range(axis_size('tp'))], axis=0), 'tp...]
    psum x1, waiting for transfers between devices: 65.8 us -> 85.8 us  [per_device(): lax.psum(grad_k[3 * tok:].astype(jnp.bfloat16), 'sp').astype(jnp.float32)]
    all_gather x1 -> x0, waiting for transfers between devices: 11.3 us -> none  [per_device(): full_grad = lax.all_gather(grad_out[0], 'tp', axis=1, tiled=True)]
    all_to_all x0 -> x1, starting transfers between devices: none -> 8.7 us  [do_blocks(): all_to_all(jnp.stack([mine for _ in range(axis_size('tp'))], axis=0), 'tp...]
    unnamed x90 -> x108, local copies, waits for them, and re-layouts: 14.2 us -> 19.6 us
where the time goes in v1:
time: 298 us; the launch traced here: 297 us
  waiting for transfers between devices  155 us (52%)
  starting transfers between devices  40 us (13%)
  local copies, waits for them, and re-layouts  37.1 us (12%)
  matrix products  24.6 us (8%)
  other arithmetic  24.5 us (8%)
  between operations  15.3 us (5%)
    psum x1, waiting for transfers between devices, per_device(): lax.psum(grad_k[3 * tok:].astype(jnp.bfloat16), 'sp').astype(jnp.float32)  85.8 us
    all_to_all x1, waiting for transfers between devices, do_blocks(): all_to_all(jnp.stack([mine for _ in range(axis_size('tp'))], axis=0), 'tp...  32.8 us
    all_to_all x2, waiting for transfers between devices, from_everyone(): return lax.all_to_all(copies, axis, split_axis=0, concat_axis=0, tiled=True)  20.9 us
    unnamed x108, local copies, waits for them, and re-layouts  19.6 us
    all_to_all x1, waiting for transfers between devices, summed_on_arrival(): parts = lax.all_to_all(cut_along(shard, dim, count), axis, 0, 0, tiled=True)  15.7 us
    all_to_all x2, starting transfers between devices, from_everyone(): return lax.all_to_all(copies, axis, split_axis=0, concat_axis=0, tiled=True)  11.5 us
    all_to_all x1, starting transfers between devices, do_blocks(): all_to_all(jnp.stack([mine for _ in range(axis_size('tp'))], axis=0), 'tp...  8.7 us
    all_to_all x1, starting transfers between devices, summed_on_arrival(): parts = lax.all_to_all(cut_along(shard, dim, count), axis, 0, 0, tiled=True)  7.29 us
  transfers between devices with their start and end apart: 9, of which 4 were waited for; matrix products, arithmetic and copies ran while one was open for 19% of the time, Pallas kernels for 0%

profile of v1, /device:TPU:32, one launch (start us, length us, event | category | flops | bytes accessed | tf_op | source)
XLA Modules:
  0.0 296.6 jit_solution(4811717579091327066)
XLA Ops:
  7.2 1.0 constant_dynamic-update-slice_fusion.1
  8.2 1.0 constant_dynamic-update-slice_fusion
  9.2 1.3 collective-permute-start.1
  10.5 5.4 %collective-permute-start = (bf16[2,384,384]{2,1,0:T(8,128)(2,1)S(1)}, bf16[2,384,384]{2,1,0:T(8,128)(2,1)}, u32[]{:S(2)}, u32[]{:S(2)}) collective-permute-start(bf16[2,384,384]{2,1,0:T(8,128)(2,1)S(1)} %constant_dynamic-update-slice_fusion), channel_id=1, source_target_pairs={{0,8},{8,16},{16,24},{24,32},{32,40},{40,48},{48,56},{1,9},{9,17},... | collective-permute-start | bytes 1769480 | tf_op jit(solution)/shard_map/ppermute | solution.py:41
  15.8 1.2 copy.25
  17.0 1.7 stack.31
  18.7 8.7 %all-to-all-start = ((bf16[8,384,384]{1,2,0:T(8,128)(2,1)}), bf16[8,384,384]{1,2,0:T(8,128)(2,1)S(1)}, u32[]{:S(2)}, u32[]{:S(2)}) async-start(bf16[8,384,384]{1,2,0:T(8,128)(2,1)} %stack.31), calls=%async_computation | async-start | bytes 4718592 | tf_op jit(solution)/shard_map/all_to_all | solution.py:12
  29.8 2.0 fusion.56
  32.5 1.4 copy.26
  34.5 0.7 reshape.152
  35.8 0.9 fusion.75
  36.8 1.6 fusion.74
  38.4 1.4 pad_maximum_fusion.2
  42.7 1.0 copy-done.5
  44.3 1.4 copy-done
  46.1 0.9 fusion.72
  47.7 0.7 copy-done.13
  48.4 1.1 convolution_convert_fusion.3
  49.4 32.8 %all-to-all-done = bf16[8,384,384]{1,2,0:T(8,128)(2,1)S(1)} async-done(((bf16[8,384,384]{1,2,0:T(8,128)(2,1)}), bf16[8,384,384]{1,2,0:T(8,128)(2,1)S(1)}, u32[]{:S(2)}, u32[]{:S(2)}) %all-to-all-start) | async-done | bytes 2359328 | tf_op jit(solution)/shard_map/all_to_all | solution.py:12
  82.2 1.6 broadcast_in_dim.59
  83.8 4.7 %all-to-all-start.1 = ((bf16[4,384,768]{1,2,0:T(8,128)(2,1)}), bf16[4,384,768]{1,2,0:T(8,128)(2,1)}, u32[]{:S(2)}, u32[]{:S(2)}) async-start(bf16[4,384,768]{1,2,0:T(8,128)(2,1)} %broadcast_in_dim.59), calls=%async_computation.1 | async-start | bytes 4718592 | tf_op jit(solution)/shard_map/all_to_all | solution.py:26
  88.5 2.1 fusion.25
  90.7 1.0 copy-done.16
  91.7 1.1 convolution_convert_fusion.2
  92.8 1.3 fusion.27
  94.1 1.9 multiply_convert_fusion
  96.0 20.9 %all-to-all-done.1 = bf16[4,384,768]{1,2,0:T(8,128)(2,1)} async-done(((bf16[4,384,768]{1,2,0:T(8,128)(2,1)}), bf16[4,384,768]{1,2,0:T(8,128)(2,1)}, u32[]{:S(2)}, u32[]{:S(2)}) %all-to-all-start.1) | async-done | bytes 2359328 | tf_op jit(solution)/shard_map/all_to_all | solution.py:26
  116.9 3.9 %convolution_convert_fusion.1 = bf16[384,384]{0,1:T(8,128)(2,1)S(1)} fusion(bf16[384,3072]{0,1:T(8,128)(2,1)} %bitcast.118, bf16[384,3072]{0,1:T(8,128)(2,1)} %bitcast.13), kind=kOutput, calls=%fused_computation.38 | convolution fusion | flops 906117120 | bytes 5013504 | tf_op jit(solution)/shard_map/dot_general | solution.py:123
  121.3 0.9 copy-done.14
  122.1 1.3 fusion.50
  123.5 1.3 fusion.53
  126.0 1.0 copy-done.4
  127.2 1.6 fusion.11
  128.8 2.2 convolution_multiply_fusion.3
  131.5 1.4 convolution_convert_fusion
  132.9 2.5 copy.30
  135.4 7.3 %all-to-all-start.2 = ((bf16[32,384,96]{1,2,0:T(8,128)(2,1)}), bf16[32,384,96]{1,2,0:T(8,128)(2,1)S(1)}, u32[]{:S(2)}, u32[]{:S(2)}) async-start(bf16[32,384,96]{1,2,0:T(8,128)(2,1)} %bitcast.117), calls=%async_computation.2 | async-start | bytes 4718592 | tf_op jit(solution)/shard_map/all_to_all | solution.py:64
  142.7 1.6 fusion.70
  144.4 1.4 convolution_multiply_fusion.4
  145.8 1.6 fusion.12
  147.4 1.0 copy-done.18
  148.4 1.4 convolution_multiply_fusion.5
  150.0 0.8 slice_bitcast_fusion.8
  150.9 0.9 pad_maximum_fusion.4
  151.8 4.6 %collective-permute-start.3 = (bf16[2,384,384]{1,2,0:T(8,128)(2,1)}, bf16[2,384,384]{1,2,0:T(8,128)(2,1)}, u32[]{:S(2)}, u32[]{:S(2)}) collective-permute-start(bf16[2,384,384]{1,2,0:T(8,128)(2,1)} %pad_maximum_fusion.4), channel_id=1, source_target_pairs={{0,8},{8,16},{16,24},{24,32},{32,40},{40,48},{48,56},{1,9},{9,17},... | collective-permute-start | bytes 1769480 | tf_op jit(solution)/shard_map/ppermute | solution.py:53
  156.8 1.1 fusion.23
  157.9 0.8 slice_bitcast_fusion.10
  158.7 15.7 %all-to-all-done.2 = bf16[32,384,96]{1,2,0:T(8,128)(2,1)S(1)} async-done(((bf16[32,384,96]{1,2,0:T(8,128)(2,1)}), bf16[32,384,96]{1,2,0:T(8,128)(2,1)S(1)}, u32[]{:S(2)}, u32[]{:S(2)}) %all-to-all-start.2) | async-done | bytes 2359328 | tf_op jit(solution)/shard_map/all_to_all | solution.py:64
  174.7 1.1 broadcast_in_dim.64
  175.8 6.8 %all-to-all-start.3 = ((f32[8,384,96]{1,2,0:T(8,128)}), f32[8,384,96]{1,2,0:T(8,128)}, u32[]{:S(2)}, u32[]{:S(2)}) async-start(f32[8,384,96]{1,2,0:T(8,128)} %broadcast_in_dim.64), calls=%async_computation.3 | async-start | bytes 2359296 | tf_op jit(solution)/shard_map/all_to_all | solution.py:26
  182.6 2.0 pad_maximum_fusion.3
  184.6 1.3 collective-permute-start.2
  185.9 1.7 fusion.24
  187.7 0.9 copy.31
  188.6 3.6 %pad_maximum_fusion = (f32[1408,384]{0,1:T(8,128)}, f32[1408,384]{0,1:T(8,128)}) fusion(f32[1408,128]{0,1:T(8,128)S(1)} %copy-done.10, f32[1408,128]{0,1:T(8,128)} %copy-done.11, f32[1408,128]{0,1:T(8,128)} %copy-done.12, f32[1408,128]{0,1:T(8,128)S(1)} %fusion.47, f32[1408,128]{0,1:T(8,128)S(1)} %copy-done.7, f32[1408,128]{0,1:T(8,128)S(1)} %copy-done.8), kind=kLoop, calls=%fused_computation.26 | loop fusion | flops 2162688 | bytes 8650752 | tf_op jit(solution)/shard_map/concatenate | solution.py:158
  192.3 85.8 %all-reduce.3.cloned.1.call-done = (bf16[1,256,384]{1,2,0:T(8,128)(2,1)}, bf16[1,256,384]{1,2,0:T(8,128)(2,1)}) async-done(((bf16[1,256,384]{1,2,0:T(8,128)(2,1)}, bf16[1,256,384]{1,2,0:T(8,128)(2,1)}), (bf16[1,256,384]{1,2,0:T(8,128)(2,1)}, bf16[1,256,384]{1,2,0:T(8,128)(2,1)})) %all-reduce.3.cloned.1.call-update) | async-done | bytes 393232 | tf_op jit(solution)/shard_map/psum | solution.py:167
  278.0 1.7 copy.34
  279.7 1.7 copy.35
  281.5 1.1 convert_element_type.132
  282.6 1.1 convert_element_type.131
  283.8 1.5 fusion.35
  285.3 0.9 copy.32
  286.2 0.9 copy.33
  287.1 2.7 copy.36
  (126 shorter events, 11.6 us)
Async XLA Ops:
  9.2 29.2 %collective-permute-start.1 = (bf16[2,384,384]{2,1,0:T(8,128)(2,1)S(1)}, bf16[2,384,384]{2,1,0:T(8,128)(2,1)}, u32[]{:S(2)}, u32[]{:S(2)}) collective-permute-start(bf16[2,384,384]{2,1,0:T(8,128)(2,1)S(1)} %constant_dynamic-update-slice_fusion), channel_id=1, source_target_pairs={{8,0},{16,8},{24,16},{32,24},{40,32},{48,40},{56,48},{9,1},{17,9},... | collective-permute-start | bytes 1769480 | tf_op jit(solution)/shard_map/ppermute | solution.py:43
  10.5 27.9 %collective-permute-start = (bf16[2,384,384]{2,1,0:T(8,128)(2,1)S(1)}, bf16[2,384,384]{2,1,0:T(8,128)(2,1)}, u32[]{:S(2)}, u32[]{:S(2)}) collective-permute-start(bf16[2,384,384]{2,1,0:T(8,128)(2,1)S(1)} %constant_dynamic-update-slice_fusion), channel_id=1, source_target_pairs={{0,8},{8,16},{16,24},{24,32},{32,40},{40,48},{48,56},{1,9},{9,17},... | collective-permute-start | bytes 1769480 | tf_op jit(solution)/shard_map/ppermute | solution.py:41
  18.7 8.7 %copy-start.44 = (bf16[1,3072]{1,0:T(2,128)(2,1)S(1)}, bf16[1,3072]{1,0:T(2,128)(2,1)}, u32[]{:S(2)}) copy-start(bf16[1,3072]{1,0:T(2,128)(2,1)} %param.17) | copy-start | bytes 18436
  18.7 9.9 %copy-start.46 = (s32[1,2]{1,0:T(1,128)S(1)}, s32[1,2]{1,0:T(1,128)}, u32[]{:S(2)}) copy-start(s32[1,2]{1,0:T(1,128)} %param.19) | copy-start | bytes 28
  18.7 10.5 %copy-start.47 = (s32[8,1]{0,1:T(1,128)S(1)}, s32[8,1]{0,1:T(1,128)}, u32[]{:S(2)}) copy-start(s32[8,1]{0,1:T(1,128)} %param.20) | copy-start | bytes 100
  18.7 63.5 %all-to-all-start = ((bf16[8,384,384]{1,2,0:T(8,128)(2,1)}), bf16[8,384,384]{1,2,0:T(8,128)(2,1)S(1)}, u32[]{:S(2)}, u32[]{:S(2)}) async-start(bf16[8,384,384]{1,2,0:T(8,128)(2,1)} %stack.31), calls=%async_computation | async-start | bytes 4718592 | tf_op jit(solution)/shard_map/all_to_all | solution.py:12
  36.8 3.5 %copy-start.36 = (bf16[256,128]{1,0:T(8,128)(2,1)}, bf16[256,128]{1,0:T(8,128)(2,1)S(1)}, u32[]{:S(2)}) copy-start(bf16[256,128]{1,0:T(8,128)(2,1)S(1)} %get-tuple-element.41) | copy-start | bytes 196612
  36.8 5.0 %copy-start.38 = (bf16[256,128]{1,0:T(8,128)(2,1)}, bf16[256,128]{1,0:T(8,128)(2,1)S(1)}, u32[]{:S(2)}) copy-start(bf16[256,128]{1,0:T(8,128)(2,1)S(1)} %get-tuple-element.40) | copy-start | bytes 196612
  36.8 7.0 %copy-start.34 = (bf16[256,128]{1,0:T(8,128)(2,1)}, bf16[256,128]{1,0:T(8,128)(2,1)S(1)}, u32[]{:S(2)}) copy-start(bf16[256,128]{1,0:T(8,128)(2,1)S(1)} %get-tuple-element.42) | copy-start | bytes 196612
  38.4 9.0 %copy-start.41 = (bf16[256,128]{1,0:T(8,128)(2,1)}, bf16[256,128]{1,0:T(8,128)(2,1)S(1)}, u32[]{:S(2)}) copy-start(bf16[256,128]{1,0:T(8,128)(2,1)S(1)} %get-tuple-element.38) | copy-start | bytes 196612
  39.9 1.0 copy-start.31
  40.2 1.5 copy-start.23
  40.2 1.5 copy-start.25
  40.2 3.5 %copy-start.22 = (bf16[1152,128]{1,0:T(8,128)(2,1)}, bf16[1152,128]{1,0:T(8,128)(2,1)S(1)}, u32[]{:S(2)}) copy-start(bf16[1152,128]{1,0:T(8,128)(2,1)S(1)} %get-tuple-element.36) | copy-start | bytes 884740
  41.4 5.6 %copy-start.3 = (f32[384,1408]{0,1:T(8,128)}, f32[384,1408]{0,1:T(8,128)S(1)}, u32[]{:S(2)}) copy-start(f32[384,1408]{0,1:T(8,128)S(1)} %get-tuple-element.48) | copy-start | bytes 6488068
  42.3 1.4 copy-start.5
  44.3 1.4 copy-start
  47.0 0.7 copy-start.27
  47.4 1.0 copy-start.13
  83.8 33.0 %all-to-all-start.1 = ((bf16[4,384,768]{1,2,0:T(8,128)(2,1)}), bf16[4,384,768]{1,2,0:T(8,128)(2,1)}, u32[]{:S(2)}, u32[]{:S(2)}) async-start(bf16[4,384,768]{1,2,0:T(8,128)(2,1)} %broadcast_in_dim.59), calls=%async_computation.1 | async-start | bytes 4718592 | tf_op jit(solution)/shard_map/all_to_all | solution.py:26
  88.5 3.2 %copy-start.29 = (bf16[1152,128]{1,0:T(8,128)(2,1)S(1)}, bf16[1152,128]{1,0:T(8,128)(2,1)}, u32[]{:S(2)}) copy-start(bf16[1152,128]{1,0:T(8,128)(2,1)} %get-tuple-element.31) | copy-start | bytes 884740
  88.5 3.2 %copy-start.43 = (bf16[256,128]{1,0:T(8,128)(2,1)S(1)}, bf16[256,128]{1,0:T(8,128)(2,1)}, u32[]{:S(2)}) copy-start(bf16[256,128]{1,0:T(8,128)(2,1)} %get-tuple-element.37) | copy-start | bytes 196612
  88.5 4.2 %copy-start.1 = (f32[384,1408]{0,1:T(8,128)S(1)}, f32[384,1408]{0,1:T(8,128)}, u32[]{:S(2)}) copy-start(f32[384,1408]{0,1:T(8,128)} %copy-done) | copy-start | bytes 6488068
  90.7 1.0 copy-start.16
  91.7 2.4 copy-start.45
  116.9 3.9 %copy-start.17 = (bf16[384,1408]{0,1:T(8,128)(2,1)S(1)}, bf16[384,1408]{0,1:T(8,128)(2,1)}, u32[]{:S(2)}) copy-start(bf16[384,1408]{0,1:T(8,128)(2,1)} %copy-done.16) | copy-start | bytes 3244036
  120.8 5.2 %copy-start.32 = (bf16[384,384]{0,1:T(8,128)(2,1)}, bf16[384,384]{0,1:T(8,128)(2,1)S(1)}, u32[]{:S(2)}) copy-start(bf16[384,384]{0,1:T(8,128)(2,1)S(1)} %convolution_convert_fusion.1) | copy-start | bytes 884740
  120.8 1.3 copy-start.14
  120.8 2.6 copy-start.15
  122.1 2.6 copy-start.40
  122.1 2.6 copy-start.48
  122.1 2.6 copy-start.49
  123.4 1.9 copy-start.6
  123.5 1.9 copy-start.30
  125.3 1.6 copy-start.4
  125.3 1.9 copy-start.28
  125.3 1.9 copy-start.42
  125.9 2.9 copy-start.19
  135.4 38.9 %all-to-all-start.2 = ((bf16[32,384,96]{1,2,0:T(8,128)(2,1)}), bf16[32,384,96]{1,2,0:T(8,128)(2,1)S(1)}, u32[]{:S(2)}, u32[]{:S(2)}) async-start(bf16[32,384,96]{1,2,0:T(8,128)(2,1)} %bitcast.117), calls=%async_computation.2 | async-start | bytes 4718592 | tf_op jit(solution)/shard_map/all_to_all | solution.py:64
  142.7 1.7 copy-start.21
  142.7 3.0 %copy-start.2 = (f32[384,1408]{0,1:T(8,128)S(1)}, f32[384,1408]{0,1:T(8,128)}, u32[]{:S(2)}) copy-start(f32[384,1408]{0,1:T(8,128)} %copy-done) | copy-start | bytes 6488068
  145.7 4.1 %copy-start.11 = (f32[1408,128]{0,1:T(8,128)}, f32[1408,128]{0,1:T(8,128)S(1)}, u32[]{:S(2)}) copy-start(f32[1408,128]{0,1:T(8,128)S(1)} %convolution_multiply_fusion.4) | copy-start | bytes 2162692
  147.4 1.0 copy-start.18
  148.4 1.5 copy-start.9
  149.8 1.0 copy-start.12
  150.0 6.4 %copy-start.20 = (bf16[384,1408]{0,1:T(8,128)(2,1)S(1)}, bf16[384,1408]{0,1:T(8,128)(2,1)}, u32[]{:S(2)}) copy-start(bf16[384,1408]{0,1:T(8,128)(2,1)} %copy-done.19) | copy-start | bytes 3244036
  150.0 6.4 %copy-start.26 = (bf16[1152,128]{1,0:T(8,128)(2,1)S(1)}, bf16[1152,128]{1,0:T(8,128)(2,1)}, u32[]{:S(2)}) copy-start(bf16[1152,128]{1,0:T(8,128)(2,1)} %copy-done.25) | copy-start | bytes 884740
  150.0 6.4 %copy-start.39 = (bf16[256,128]{1,0:T(8,128)(2,1)S(1)}, bf16[256,128]{1,0:T(8,128)(2,1)}, u32[]{:S(2)}) copy-start(bf16[256,128]{1,0:T(8,128)(2,1)} %copy-done.38) | copy-start | bytes 196612
  150.0 6.8 %copy-start.24 = (bf16[1152,128]{1,0:T(8,128)(2,1)S(1)}, bf16[1152,128]{1,0:T(8,128)(2,1)}, u32[]{:S(2)}) copy-start(bf16[1152,128]{1,0:T(8,128)(2,1)} %copy-done.23) | copy-start | bytes 884740
  150.0 6.8 %copy-start.37 = (bf16[256,128]{1,0:T(8,128)(2,1)S(1)}, bf16[256,128]{1,0:T(8,128)(2,1)}, u32[]{:S(2)}) copy-start(bf16[256,128]{1,0:T(8,128)(2,1)} %copy-done.36) | copy-start | bytes 196612
  151.8 129.7 %collective-permute-start.3 = (bf16[2,384,384]{1,2,0:T(8,128)(2,1)}, bf16[2,384,384]{1,2,0:T(8,128)(2,1)}, u32[]{:S(2)}, u32[]{:S(2)}) collective-permute-start(bf16[2,384,384]{1,2,0:T(8,128)(2,1)} %pad_maximum_fusion.4), channel_id=1, source_target_pairs={{0,8},{8,16},{16,24},{24,32},{32,40},{40,48},{48,56},{1,9},{9,17},... | collective-permute-start | bytes 1769480 | tf_op jit(solution)/shard_map/ppermute | solution.py:53
  174.7 11.3 %copy-start.35 = (bf16[256,128]{1,0:T(8,128)(2,1)S(1)}, bf16[256,128]{1,0:T(8,128)(2,1)}, u32[]{:S(2)}) copy-start(bf16[256,128]{1,0:T(8,128)(2,1)} %copy-done.34) | copy-start | bytes 196612
  175.8 111.3 %all-to-all-start.3 = ((f32[8,384,96]{1,2,0:T(8,128)}), f32[8,384,96]{1,2,0:T(8,128)}, u32[]{:S(2)}, u32[]{:S(2)}) async-start(f32[8,384,96]{1,2,0:T(8,128)} %broadcast_in_dim.64), calls=%async_computation.3 | async-start | bytes 2359296 | tf_op jit(solution)/shard_map/all_to_all | solution.py:26
  182.6 5.1 %copy-start.33 = (bf16[1,384,128]{1,2,0:T(8,128)(2,1)S(1)}, bf16[1,384,128]{1,2,0:T(8,128)(2,1)}, u32[]{:S(2)}) copy-start(bf16[1,384,128]{1,2,0:T(8,128)(2,1)} %fusion.23) | copy-start | bytes 294916
  182.6 95.4 %all-reduce.3.cloned.1.call-start = ((), (), s32[]{:S(2)}) async-start(), calls=%async_computation.4 | async-start | bytes 786432 | tf_op jit(solution)/shard_map/psum | solution.py:167
  182.6 6.0 %copy-start.7 = (f32[1408,128]{0,1:T(8,128)S(1)}, f32[1408,128]{0,1:T(8,128)}, u32[]{:S(2)}) copy-start(f32[1408,128]{0,1:T(8,128)} %fusion.50) | copy-start | bytes 2162692
  182.6 6.0 %copy-start.8 = (f32[1408,128]{0,1:T(8,128)S(1)}, f32[1408,128]{0,1:T(8,128)}, u32[]{:S(2)}) copy-start(f32[1408,128]{0,1:T(8,128)} %fusion.53) | copy-start | bytes 2162692
  182.6 6.0 %copy-start.10 = (f32[1408,128]{0,1:T(8,128)S(1)}, f32[1408,128]{0,1:T(8,128)}, u32[]{:S(2)}) copy-start(f32[1408,128]{0,1:T(8,128)} %convolution_multiply_fusion.3) | copy-start | bytes 2162692
  184.6 98.0 %collective-permute-start.2 = (bf16[2,384,384]{1,2,0:T(8,128)(2,1)}, bf16[2,384,384]{1,2,0:T(8,128)(2,1)}, u32[]{:S(2)}, u32[]{:S(2)}) collective-permute-start(bf16[2,384,384]{1,2,0:T(8,128)(2,1)} %pad_maximum_fusion.3), channel_id=1, source_target_pairs={{8,0},{16,8},{24,16},{32,24},{40,32},{48,40},{56,48},{9,1},{17,9},... | collective-permute-start | bytes 1769480 | tf_op jit(solution)/shard_map/ppermute | solution.py:53
Sparse Core Ops, SparseCore 0:
  187.8 90.1 all-reduce.2
